TPU v7x, 32 devices: a whole 2x2x4 slice. The times are simulated.
32 devices in a mesh: shard: 8 (over z, x), rep: 4 (over y, core).
Axes of the slice: x: 2, y: 2, z: 4, core: 2. Of those that a mesh axis runs over, the one named last changes fastest.
Arguments:
- lender_block: int32 [96, 8], P(('shard', 'rep')), may hold values from 0 to 255, as said below
- confidence: bfloat16 [96, 8, 256, 256], P(('shard', 'rep')), may hold values from 0 to 80, as said below
- lender_factors: bfloat16 [65536, 128], P('shard'), may hold values from -4 to 4
Outputs:
- borrower_factors: float32 [24576, 128], P(('shard', 'rep'))
- lender_rhs: float32 [65536, 128], P('shard')
Inputs may be any that keep to these rules, and one draw needn't show every extreme that they name: `lender_block`: within one device's 3 borrower blocks, at most 6 of the 3 x 8 entries name blocks of any one owner (block // 32), and on every device some owner is named exactly 6 times. `confidence`: about half the entries are zero; the others are positive.
All inputs are finite; a program needn't handle non-finite values.
Results may differ from a plain program's by a relative error of at most 0.0047.
Values may be sent and summed in bfloat16 or wider, within the bound.
A program may use at most 128 MiB of HBM per device.

v0:
```python
import jax
import jax.numpy as jnp
from jax import lax
from jax.sharding import PartitionSpec as P

CG_STEPS = 3
HIGH = lax.Precision.HIGHEST


def apply_system(direction, confidence, fetched, gram):
    low = direction.astype(jnp.bfloat16)
    scores = jnp.einsum("btr,bklr->bktl", low, fetched, preferred_element_type=jnp.float32)
    weighted = (confidence.astype(jnp.float32) * scores).astype(jnp.bfloat16)
    back = jnp.einsum("bktl,bklr->btr", weighted, fetched, preferred_element_type=jnp.float32)
    width = direction.shape[-1]
    global_part = jnp.dot(
        direction.reshape(-1, width), gram, precision=HIGH, preferred_element_type=jnp.float32
    )
    return global_part.reshape(direction.shape) + 0.1 * direction + back


def per_device(lender_block, confidence, lender_factors):
    shards = lax.axis_size("shard")
    blocks, lists = lender_block.shape
    tile = confidence.shape[2]
    rank = lender_factors.shape[1]
    owned = lender_factors.shape[0] // tile
    entries = blocks * lists
    slots = (2 * entries + shards - 1) // shards
    local_gram = lax.dot_general(
        lender_factors, lender_factors, (((0,), (0,)), ((), ())), preferred_element_type=jnp.float32
    )
    gram = lax.psum(local_gram, "shard")
    flat = lender_block.reshape(entries)
    owner = flat // owned
    within = flat - owner * owned
    member = (owner[:, None] == jnp.arange(shards, dtype=jnp.int32)[None, :]).astype(jnp.int32)
    position = jnp.sum(jnp.cumsum(member, axis=0) * member, axis=1) - 1
    slot_index = owner * slots + position
    requests = (
        jnp.zeros((shards * slots,), jnp.int32).at[slot_index].set(within).reshape(shards, slots)
    )
    table = lender_factors.reshape(owned, tile, rank)
    incoming = lax.all_to_all(requests, "shard", split_axis=0, concat_axis=0, tiled=True)
    replies = lax.all_to_all(table[incoming], "shard", split_axis=0, concat_axis=0, tiled=True)
    fetched = replies.reshape(shards * slots, tile, rank)[slot_index].reshape(
        blocks, lists, tile, rank
    )
    rhs = jnp.einsum("bktl,bklr->btr", confidence, fetched, preferred_element_type=jnp.float32)
    solution = jnp.zeros_like(rhs)
    resid = rhs
    direction = rhs
    norm_now = jnp.sum(resid * resid, axis=2, keepdims=True)
    for count in range(CG_STEPS):
        image = apply_system(direction, confidence, fetched, gram)
        alpha = norm_now / (jnp.sum(direction * image, axis=2, keepdims=True) + 1e-06)
        solution = solution + alpha * direction
        resid = resid - alpha * image
        norm_next = jnp.sum(resid * resid, axis=2, keepdims=True)
        direction = resid + norm_next / (norm_now + 1e-06) * direction
        norm_now = norm_next
    solved = solution.astype(jnp.bfloat16)
    partial_rhs = jnp.einsum(
        "bktl,btr->bklr", confidence, solved, preferred_element_type=jnp.float32
    )
    outgoing = (
        jnp.zeros((shards * slots, tile, rank), jnp.float32)
        .at[slot_index]
        .set(partial_rhs.reshape(entries, tile, rank))
    )
    returned = lax.all_to_all(
        outgoing.reshape(shards, slots, tile, rank),
        "shard",
        split_axis=0,
        concat_axis=0,
        tiled=True,
    )
    selector = (
        incoming.reshape(-1)[None, :] == jnp.arange(owned, dtype=jnp.int32)[:, None]
    ).astype(jnp.float32)
    owner_sum = jnp.dot(
        selector,
        returned.reshape(shards * slots, tile * rank),
        precision=HIGH,
        preferred_element_type=jnp.float32,
    )
    total = lax.psum(owner_sum, "rep")
    lenders_all = owned * tile * shards
    lender_rhs = total.reshape(owned * tile, rank) / lenders_all
    return (solution.reshape(blocks * tile, rank), lender_rhs)


def solution(mesh):
    in_specs = (P(("shard", "rep"), None), P(("shard", "rep"), None, None, None), P("shard", None))
    out_specs = (P(("shard", "rep"), None), P("shard", None))
    return jax.shard_map(
        per_device, mesh=mesh, in_specs=in_specs, out_specs=out_specs, check_vma=False
    )
```

profile of v0, /device:TPU:0, one launch (start us, length us, event | category | flops | bytes accessed | tf_op | source)
XLA Modules:
  0.0 416.2 jit_solution(9014133852448018927)
XLA Ops:
  7.2 0.9 reshape.224
  8.1 0.8 reshape.223
  9.2 0.6 scatter_custom_fusion
  9.9 13.6 %all_to_all.22 = s32[8,1,6]{2,1,0:T(1,128)S(1)} all-to-all(s32[8,1,6]{2,1,0:T(1,128)S(1)} %bitcast.112), channel_id=1, replica_groups=mesh['shard'=8,'rep'=4] {'shard'}, dimensions={0} | all-to-all | bytes 384 | tf_op jit(solution)/shard_map/all_to_all | solution.py:44
  23.8 2.7 gather_fusion
  26.5 4.4 %all-to-all-start.1 = ((bf16[8,6,256,128]{3,2,1,0:T(8,128)(2,1)}), bf16[8,6,256,128]{3,2,1,0:T(8,128)(2,1)}, u32[]{:S(2)}, u32[]{:S(2)}) async-start(bf16[8,6,256,128]{3,2,1,0:T(8,128)(2,1)} %bitcast.106), calls=%async_computation.1 | async-start | bytes 6291456 | tf_op jit(solution)/shard_map/all_to_all | solution.py:45
  31.0 1.4 fusion.55
  32.4 4.7 %copy.37 = bf16[3,8,256,256]{2,3,1,0:T(8,128)(2,1)} copy(bf16[3,8,256,256]{3,2,1,0:T(8,128)(2,1)} %param.4) | data formatting | bytes 6291456 | tf_op args[1]
  37.1 64.9 %all-to-all-done.1 = bf16[8,6,256,128]{3,2,1,0:T(8,128)(2,1)} async-done(((bf16[8,6,256,128]{3,2,1,0:T(8,128)(2,1)}), bf16[8,6,256,128]{3,2,1,0:T(8,128)(2,1)}, u32[]{:S(2)}, u32[]{:S(2)}) %all-to-all-start.1) | async-done | bytes 3145760 | tf_op jit(solution)/shard_map/all_to_all | solution.py:45
  102.0 3.8 gather_fusion.1
  105.8 3.5 convolution_bitcast_fusion
  109.4 4.3 %fusion.18 = f32[3,256,128]{1,2,0:T(8,128)S(1)} fusion(bf16[3,8,256,128]{3,2,1,0:T(8,128)(2,1)} %bitcast.108, bf16[3,8,256,256]{2,3,1,0:T(8,128)(2,1)} %copy.37, f32[3,256,128]{1,2,0:T(8,128)S(1)} %convolution_bitcast_fusion), kind=kOutput, calls=%fused_computation.20 | convolution fusion | flops 810123264 | bytes 5505024 | tf_op jit(solution)/shard_map/bktl,bklr->btr/dot_general | solution.py:14
  113.7 13.5 %all-reduce.3.cloned.1.call-done = f32[128,128]{1,0:T(8,128)} async-done(((f32[128,128]{1,0:T(8,128)}), f32[128,128]{1,0:T(8,128)}) %all-reduce.3.cloned.1.call-update) | async-done | bytes 65552 | tf_op jit(solution)/shard_map/psum | solution.py:33
  127.2 1.4 multiply_reduce_fusion.3
  128.8 5.1 %fusion.21 = f32[3,256,128]{1,2,0:T(8,128)} fusion(bf16[3,8,256,128]{3,2,1,0:T(8,128)(2,1)} %bitcast.109, bf16[3,8,256,256]{2,3,1,0:T(8,128)(2,1)} %copy.37, f32[3,256,128]{1,2,0:T(8,128)S(1)} %multiply_add_fusion.2), kind=kOutput, calls=%fused_computation.21 | convolution fusion | flops 810123264 | bytes 5505024 | tf_op jit(solution)/shard_map/bktl,bklr->btr/dot_general | solution.py:14
  133.8 1.6 multiply_reduce_fusion.1
  135.5 0.8 multiply_add_fusion.1
  136.3 5.2 %fusion.24 = f32[3,256,128]{1,2,0:T(8,128)} fusion(bf16[3,8,256,128]{3,2,1,0:T(8,128)(2,1)} %bitcast.110, bf16[3,8,256,256]{2,3,1,0:T(8,128)(2,1)} %copy.37, f32[3,256,128]{1,2,0:T(8,128)} %multiply_add_fusion.1), kind=kOutput, calls=%fused_computation.22 | convolution fusion | flops 810123264 | bytes 5505024 | tf_op jit(solution)/shard_map/bktl,bklr->btr/dot_general | solution.py:14
  141.5 1.6 fusion.31
  143.1 1.1 multiply_add_fusion
  144.2 4.1 fusion.38
  148.3 3.6 copy.52
  151.9 3.4 broadcast_in_dim.5
  155.3 7.9 %scatter_fusion = f32[48,256,128]{2,1,0:T(8,128)} fusion(f32[48,256,128]{2,1,0:T(8,128)} %broadcast_in_dim.5, s32[24]{0:T(128)S(1)} %fusion.52, f32[24,256,128]{2,1,0:T(8,128)} %copy.52), kind=kCustom, calls=%fused_computation.3 | custom fusion | bytes 9437280 | tf_op jit(solution)/shard_map/scatter | solution.py:69
  163.3 4.8 %all-to-all-start.2 = ((f32[8,6,256,128]{3,2,1,0:T(8,128)}), f32[8,6,256,128]{3,2,1,0:T(8,128)}, u32[]{:S(2)}, u32[]{:S(2)}) async-start(f32[8,6,256,128]{3,2,1,0:T(8,128)} %bitcast.104), calls=%async_computation.2 | async-start | bytes 12582912 | tf_op jit(solution)/shard_map/all_to_all | solution.py:71
  168.8 0.7 reduce.3
  169.5 135.1 %all-to-all-done.2 = f32[8,6,256,128]{3,2,1,0:T(8,128)} async-done(((f32[8,6,256,128]{3,2,1,0:T(8,128)}), f32[8,6,256,128]{3,2,1,0:T(8,128)}, u32[]{:S(2)}, u32[]{:S(2)}) %all-to-all-start.2) | async-done | bytes 6291488 | tf_op jit(solution)/shard_map/all_to_all | solution.py:71
  304.6 10.8 %fusion.3 = f32[32,32768]{1,0:T(8,128)} fusion(f32[6,8,256,128]{3,2,1,0:T(8,128)} %bitcast.40, s32[48]{0:T(128)S(1)} %eq.31), kind=kOutput, calls=%fused_computation.10 | convolution fusion | flops 603981312 | bytes 10485952 | tf_op jit(solution)/shard_map/dot_general | solution.py:81
  315.4 0.9 copy.51
  316.3 83.7 %all-reduce.5.cloned.1.call-done = f32[32,32768]{1,0:T(8,128)} async-done(((f32[32,32768]{1,0:T(8,128)}), f32[32,32768]{1,0:T(8,128)}) %all-reduce.5.cloned.1.call-update) | async-done | bytes 4194320 | tf_op jit(solution)/shard_map/psum | solution.py:87
  400.0 4.4 %broadcast_multiply_fusion = f32[32,32768]{1,0:T(8,128)} fusion(f32[32,32768]{1,0:T(8,128)} %all-reduce.5.cloned.1.call-done), kind=kLoop, calls=%fused_computation.19 | loop fusion | flops 1048576 | bytes 8388608 | tf_op jit(solution)/shard_map/div | solution.py:89
  404.5 4.9 %div.83 = f32[8192,128]{1,0:T(8,128)} reshape(f32[32,32768]{1,0:T(8,128)} %broadcast_multiply_fusion) | data formatting | bytes 8388608 | tf_op jit(solution)/shard_map/div | solution.py:89
  (32 shorter events, 1.8 us)
Async XLA Ops:
  7.2 16.6 %copy-start = (bf16[8192,128]{1,0:T(8,128)(2,1)S(1)}, bf16[8192,128]{1,0:T(8,128)(2,1)}, u32[]{:S(2)}) copy-start(bf16[8192,128]{1,0:T(8,128)(2,1)} %param.5) | copy-start | bytes 6291460
  26.5 75.5 %all-to-all-start.1 = ((bf16[8,6,256,128]{3,2,1,0:T(8,128)(2,1)}), bf16[8,6,256,128]{3,2,1,0:T(8,128)(2,1)}, u32[]{:S(2)}, u32[]{:S(2)}) async-start(bf16[8,6,256,128]{3,2,1,0:T(8,128)(2,1)} %bitcast.106), calls=%async_computation.1 | async-start | bytes 6291456 | tf_op jit(solution)/shard_map/all_to_all | solution.py:45
  30.9 96.2 %all-reduce.3.cloned.1.call-start = ((), (), s32[]{:S(2)}) async-start(), calls=%async_computation.3 | async-start | bytes 131072 | tf_op jit(solution)/shard_map/psum | solution.py:33
  128.7 5.1 %copy-start.2 = (f32[128,128]{1,0:T(8,128)S(1)}, f32[128,128]{1,0:T(8,128)}, u32[]{:S(2)}) copy-start(f32[128,128]{1,0:T(8,128)} %all-reduce.3.cloned.1.call-done) | copy-start | bytes 196612
  136.3 5.2 %copy-start.1 = (f32[3,256,128]{1,2,0:T(8,128)S(1)}, f32[3,256,128]{1,2,0:T(8,128)}, u32[]{:S(2)}) copy-start(f32[3,256,128]{1,2,0:T(8,128)} %multiply_add_fusion.1) | copy-start | bytes 1179652
  163.3 141.3 %all-to-all-start.2 = ((f32[8,6,256,128]{3,2,1,0:T(8,128)}), f32[8,6,256,128]{3,2,1,0:T(8,128)}, u32[]{:S(2)}, u32[]{:S(2)}) async-start(f32[8,6,256,128]{3,2,1,0:T(8,128)} %bitcast.104), calls=%async_computation.2 | async-start | bytes 12582912 | tf_op jit(solution)/shard_map/all_to_all | solution.py:71
  168.0 232.0 %all-reduce.5.cloned.1.call-start = ((), (), s32[]{:S(2)}) async-start(), calls=%async_computation.4 | async-start | bytes 8388608 | tf_op jit(solution)/shard_map/psum | solution.py:87
Sparse Core Ops, SparseCore 0:
  35.7 91.3 all-reduce.2
  315.5 84.4 all-reduce.4
where the time goes:
time: 417 us; the launch traced here: 416 us
  waiting for transfers between devices  297 us (71%)
  matrix products  39 us (9%)
  local copies, waits for them, and re-layouts  35.2 us (8%)
  between operations  14.2 us (3%)
  blocking collectives  13.6 us (3%)
  starting transfers between devices  9.46 us (2%)
  other arithmetic  7.59 us (2%)
    all_to_all x1, waiting for transfers between devices, per_device(): lax.all_to_all(outgoing.reshape(shards, slots, tile, rank), 'shard', spli...  135 us
    psum x1, waiting for transfers between devices, per_device(): total = lax.psum(owner_sum, 'rep')  83.7 us
    all_to_all x1, waiting for transfers between devices, per_device(): lax.all_to_all(table[incoming], 'shard', split_axis=0, concat_axis=0, til...  64.9 us
    dot_general x3, matrix products, apply_system(): jnp.einsum('bktl,bklr->btr', weighted, fetched, preferred_element_type=jn...  14.5 us
    all_to_all x1, blocking collectives, per_device(): lax.all_to_all(requests, 'shard', split_axis=0, concat_axis=0, tiled=True)  13.6 us
    psum x1, waiting for transfers between devices, per_device(): gram = lax.psum(local_gram, 'shard')  13.5 us
    dot_general x1, matrix products, per_device(): jnp.dot(selector, returned.reshape(shards * slots, tile * rank), precisio...  10.8 us
  transfers between devices with their start and end apart: 4, of which 4 were waited for; matrix products, arithmetic and copies ran while one was open for 5% of the time, Pallas kernels for 0%

commit v1 on v0

--- a/solution.py
+++ b/solution.py
@@ -41,7 +41,19 @@
         jnp.zeros((shards * slots,), jnp.int32).at[slot_index].set(within).reshape(shards, slots)
     )
     table = lender_factors.reshape(owned, tile, rank)
-    incoming = lax.all_to_all(requests, "shard", split_axis=0, concat_axis=0, tiled=True)
+    ways, here = (lax.axis_size("shard"), lax.axis_index("shard"))
+    width_2 = requests.shape[0] // ways
+    dims = list(requests.shape)
+    dims[0] = width_2
+    height = dims[0]
+    dims[0] = height * ways
+    full = jnp.zeros(dims, requests.dtype)
+    for mask in range(ways):
+        part = lax.dynamic_slice_in_dim(requests, (here ^ mask) * width_2, width_2, axis=0)
+        if mask:
+            part = lax.ppermute(part, "shard", [(d, d ^ mask) for d in range(ways)])
+        full = lax.dynamic_update_slice_in_dim(full, part, (here ^ mask) * height, axis=0)
+    incoming = full
     replies = lax.all_to_all(table[incoming], "shard", split_axis=0, concat_axis=0, tiled=True)
     fetched = replies.reshape(shards * slots, tile, rank)[slot_index].reshape(
         blocks, lists, tile, rank

time: 417 us -> 423 us (1.014)
  starting transfers between devices: 9.46 us -> 25.3 us
  blocking collectives: 13.6 us -> 0 us
  waiting for transfers between devices: 297 us -> 305 us
  local copies, waits for them, and re-layouts: 35.2 us -> 30.1 us
    ppermute x0 -> x7, starting transfers between devices: none -> 14.4 us  [per_device(): part = lax.ppermute(part, 'shard', [(d, d ^ mask) for d in range(ways)])]
    all_to_all x1 -> x0, blocking collectives: 13.6 us -> none  [per_device(): lax.all_to_all(requests, 'shard', split_axis=0, concat_axis=0, tiled=True)]
    ppermute x0 -> x7, waiting for transfers between devices: none -> 6.25 us  [per_device(): part = lax.ppermute(part, 'shard', [(d, d ^ mask) for d in range(ways)])]
    unnamed x7 -> x6, local copies, waits for them, and re-layouts: 4.71 us -> 0.02 us
  transfers between devices with their start and end apart: 4 -> 11, of which waited for: 4 -> 7; matrix products, arithmetic and copies ran while one was open for 5% -> 3% of each run, Pallas kernels for 0% -> 0%
where the time goes in v1:
time: 423 us; the launch traced here: 422 us
  waiting for transfers between devices  305 us (72%)
  matrix products  40.4 us (10%)
  local copies, waits for them, and re-layouts  30.1 us (7%)
  starting transfers between devices  25.3 us (6%)
  between operations  14.2 us (3%)
  other arithmetic  6.93 us (2%)
    all_to_all x1, waiting for transfers between devices, per_device(): lax.all_to_all(outgoing.reshape(shards, slots, tile, rank), 'shard', spli...  136 us
    psum x1, waiting for transfers between devices, per_device(): total = lax.psum(owner_sum, 'rep')  83.7 us
    all_to_all x1, waiting for transfers between devices, per_device(): lax.all_to_all(table[incoming], 'shard', split_axis=0, concat_axis=0, til...  66.5 us
    dot_general x3, matrix products, apply_system(): jnp.einsum('bktl,bklr->btr', weighted, fetched, preferred_element_type=jn...  16 us
    ppermute x7, starting transfers between devices, per_device(): part = lax.ppermute(part, 'shard', [(d, d ^ mask) for d in range(ways)])  14.4 us
    psum x1, waiting for transfers between devices, per_device(): gram = lax.psum(local_gram, 'shard')  12.1 us
    dot_general x1, matrix products, per_device(): jnp.dot(selector, returned.reshape(shards * slots, tile * rank), precisio...  10.8 us
  transfers between devices with their start and end apart: 11, of which 7 were waited for; matrix products, arithmetic and copies ran while one was open for 3% of the time, Pallas kernels for 0%

profile of v1, /device:TPU:0, one launch (start us, length us, event | category | flops | bytes accessed | tf_op | source)
XLA Modules:
  0.0 421.8 jit_solution(17701941789632341092)
XLA Ops:
  10.0 6.1 %collective-permute-start.6 = (s32[1,6]{1,0:T(1,128)S(1)}, s32[1,6]{1,0:T(1,128)S(1)}, u32[]{:S(2)}, u32[]{:S(2)}) collective-permute-start(s32[1,6]{1,0:T(1,128)S(1)} %get-tuple-element.8), channel_id=1, source_target_pairs={{0,28},{4,24},{8,20},{12,16},{16,12},{20,8},{24,4},{28,0},{1,29},{... | collective-permute-start | bytes 80 | tf_op jit(solution)/shard_map/ppermute | solution.py:54
  17.0 2.0 collective-permute-start.3
  19.1 1.6 collective-permute-start
  20.7 1.9 collective-permute-done
  22.6 1.4 collective-permute-start.1
  24.0 2.2 collective-permute-done.1
  26.2 2.3 collective-permute-start.2
  28.5 2.2 collective-permute-done.2
  31.0 2.7 gather_fusion
  33.7 5.9 %all-to-all-start = ((bf16[8,6,256,128]{3,2,1,0:T(8,128)(2,1)}), bf16[8,6,256,128]{3,2,1,0:T(8,128)(2,1)}, u32[]{:S(2)}, u32[]{:S(2)}) async-start(bf16[8,6,256,128]{3,2,1,0:T(8,128)(2,1)} %bitcast.101), calls=%async_computation | async-start | bytes 6291456 | tf_op jit(solution)/shard_map/all_to_all | solution.py:57
  39.7 1.4 fusion.55
  41.1 66.5 %all-to-all-done = bf16[8,6,256,128]{3,2,1,0:T(8,128)(2,1)} async-done(((bf16[8,6,256,128]{3,2,1,0:T(8,128)(2,1)}), bf16[8,6,256,128]{3,2,1,0:T(8,128)(2,1)}, u32[]{:S(2)}, u32[]{:S(2)}) %all-to-all-start) | async-done | bytes 3145760 | tf_op jit(solution)/shard_map/all_to_all | solution.py:57
  107.6 3.8 gather_fusion.1
  111.4 3.5 convolution_bitcast_fusion
  115.0 4.8 %fusion.18 = f32[3,256,128]{1,2,0:T(8,128)S(1)} fusion(bf16[3,8,256,128]{3,2,1,0:T(8,128)(2,1)} %bitcast.103, bf16[3,8,256,256]{3,2,1,0:T(8,128)(2,1)} %param.4, f32[3,256,128]{1,2,0:T(8,128)S(1)} %convolution_bitcast_fusion), kind=kOutput, calls=%fused_computation.20 | convolution fusion | flops 810123264 | bytes 5505024 | tf_op jit(solution)/shard_map/bktl,bklr->btr/dot_general | solution.py:14
  119.7 12.1 %all-reduce.3.cloned.1.call-done = f32[128,128]{1,0:T(8,128)} async-done(((f32[128,128]{1,0:T(8,128)}), f32[128,128]{1,0:T(8,128)}) %all-reduce.3.cloned.1.call-update) | async-done | bytes 65552 | tf_op jit(solution)/shard_map/psum | solution.py:33
  131.8 1.4 multiply_reduce_fusion.3
  133.4 5.5 %fusion.21 = f32[3,256,128]{1,2,0:T(8,128)} fusion(bf16[3,8,256,128]{3,2,1,0:T(8,128)(2,1)} %bitcast.104, bf16[3,8,256,256]{3,2,1,0:T(8,128)(2,1)} %param.4, f32[3,256,128]{1,2,0:T(8,128)S(1)} %multiply_add_fusion.2), kind=kOutput, calls=%fused_computation.21 | convolution fusion | flops 810123264 | bytes 5505024 | tf_op jit(solution)/shard_map/bktl,bklr->btr/dot_general | solution.py:14
  139.0 1.6 multiply_reduce_fusion.1
  141.5 5.7 %fusion.24 = f32[3,256,128]{1,2,0:T(8,128)} fusion(bf16[3,8,256,128]{3,2,1,0:T(8,128)(2,1)} %bitcast.105, bf16[3,8,256,256]{3,2,1,0:T(8,128)(2,1)} %param.4, f32[3,256,128]{1,2,0:T(8,128)} %multiply_add_fusion.1), kind=kOutput, calls=%fused_computation.22 | convolution fusion | flops 810123264 | bytes 5505024 | tf_op jit(solution)/shard_map/bktl,bklr->btr/dot_general | solution.py:14
  147.1 1.6 fusion.31
  148.7 1.1 multiply_add_fusion
  149.8 4.1 fusion.32
  153.9 3.6 copy.26
  157.5 3.4 broadcast_in_dim.8
  160.9 7.9 %scatter_fusion = f32[48,256,128]{2,1,0:T(8,128)} fusion(f32[48,256,128]{2,1,0:T(8,128)} %broadcast_in_dim.8, s32[24]{0:T(128)S(1)} %fusion.52, f32[24,256,128]{2,1,0:T(8,128)} %copy.26), kind=kCustom, calls=%fused_computation.3 | custom fusion | bytes 9437280 | tf_op jit(solution)/shard_map/scatter | solution.py:81
  168.9 4.8 %all-to-all-start.1 = ((f32[8,6,256,128]{3,2,1,0:T(8,128)}), f32[8,6,256,128]{3,2,1,0:T(8,128)}, u32[]{:S(2)}, u32[]{:S(2)}) async-start(f32[8,6,256,128]{3,2,1,0:T(8,128)} %bitcast.99), calls=%async_computation.1 | async-start | bytes 12582912 | tf_op jit(solution)/shard_map/all_to_all | solution.py:83
  173.9 136.2 %all-to-all-done.1 = f32[8,6,256,128]{3,2,1,0:T(8,128)} async-done(((f32[8,6,256,128]{3,2,1,0:T(8,128)}), f32[8,6,256,128]{3,2,1,0:T(8,128)}, u32[]{:S(2)}, u32[]{:S(2)}) %all-to-all-start.1) | async-done | bytes 6291488 | tf_op jit(solution)/shard_map/all_to_all | solution.py:83
  310.2 10.8 %fusion.3 = f32[32,32768]{1,0:T(8,128)} fusion(f32[6,8,256,128]{3,2,1,0:T(8,128)} %bitcast.37, s32[48]{0:T(128)S(1)} %eq.31), kind=kOutput, calls=%fused_computation.10 | convolution fusion | flops 603981312 | bytes 10485952 | tf_op jit(solution)/shard_map/dot_general | solution.py:93
  322.0 83.7 %all-reduce.5.cloned.1.call-done = f32[32,32768]{1,0:T(8,128)} async-done(((f32[32,32768]{1,0:T(8,128)}), f32[32,32768]{1,0:T(8,128)}) %all-reduce.5.cloned.1.call-update) | async-done | bytes 4194320 | tf_op jit(solution)/shard_map/psum | solution.py:99
  405.6 4.4 %broadcast_multiply_fusion = f32[32,32768]{1,0:T(8,128)} fusion(f32[32,32768]{1,0:T(8,128)} %all-reduce.5.cloned.1.call-done), kind=kLoop, calls=%fused_computation.19 | loop fusion | flops 1048576 | bytes 8388608 | tf_op jit(solution)/shard_map/div | solution.py:101
  410.1 4.9 %div.83 = f32[8192,128]{1,0:T(8,128)} reshape(f32[32,32768]{1,0:T(8,128)} %broadcast_multiply_fusion) | data formatting | bytes 8388608 | tf_op jit(solution)/shard_map/div | solution.py:101
  (50 shorter events, 6.5 us)
Async XLA Ops:
  7.2 23.8 %copy-start = (bf16[8192,128]{1,0:T(8,128)(2,1)S(1)}, bf16[8192,128]{1,0:T(8,128)(2,1)}, u32[]{:S(2)}) copy-start(bf16[8192,128]{1,0:T(8,128)(2,1)} %param.5) | copy-start | bytes 6291460
  10.0 20.8 %collective-permute-start.6 = (s32[1,6]{1,0:T(1,128)S(1)}, s32[1,6]{1,0:T(1,128)S(1)}, u32[]{:S(2)}, u32[]{:S(2)}) collective-permute-start(s32[1,6]{1,0:T(1,128)S(1)} %get-tuple-element.8), channel_id=1, source_target_pairs={{0,28},{4,24},{8,20},{12,16},{16,12},{20,8},{24,4},{28,0},{1,29},{... | collective-permute-start | bytes 80 | tf_op jit(solution)/shard_map/ppermute | solution.py:54
  16.0 14.7 %collective-permute-start.5 = (s32[1,6]{1,0:T(1,128)S(1)}, s32[1,6]{1,0:T(1,128)S(1)}, u32[]{:S(2)}, u32[]{:S(2)}) collective-permute-start(s32[1,6]{1,0:T(1,128)S(1)} %get-tuple-element.9), channel_id=1, source_target_pairs={{0,24},{4,28},{8,16},{12,20},{16,8},{20,12},{24,0},{28,4},{1,25},{... | collective-permute-start | bytes 80 | tf_op jit(solution)/shard_map/ppermute | solution.py:54
  16.3 14.5 %collective-permute-start.4 = (s32[1,6]{1,0:T(1,128)S(1)}, s32[1,6]{1,0:T(1,128)S(1)}, u32[]{:S(2)}, u32[]{:S(2)}) collective-permute-start(s32[1,6]{1,0:T(1,128)S(1)} %get-tuple-element.10), channel_id=1, source_target_pairs={{0,20},{4,16},{8,28},{12,24},{16,4},{20,0},{24,12},{28,8},{1,21},{... | collective-permute-start | bytes 80 | tf_op jit(solution)/shard_map/ppermute | solution.py:54
  17.0 13.7 %collective-permute-start.3 = (s32[1,6]{1,0:T(1,128)S(1)}, s32[1,6]{1,0:T(1,128)S(1)}, u32[]{:S(2)}, u32[]{:S(2)}) collective-permute-start(s32[1,6]{1,0:T(1,128)S(1)} %get-tuple-element.11), channel_id=1, source_target_pairs={{0,16},{4,20},{8,24},{12,28},{16,0},{20,4},{24,8},{28,12},{1,17},{... | collective-permute-start | bytes 80 | tf_op jit(solution)/shard_map/ppermute | solution.py:54
  19.1 3.6 collective-permute-start
  22.6 3.6 collective-permute-start.1
  26.2 4.5 %collective-permute-start.2 = (s32[1,6]{1,0:T(1,128)S(1)}, s32[1,6]{1,0:T(1,128)S(1)}, u32[]{:S(2)}, u32[]{:S(2)}) collective-permute-start(s32[1,6]{1,0:T(1,128)S(1)} %get-tuple-element.12), channel_id=1, source_target_pairs={{0,12},{4,8},{8,4},{12,0},{16,28},{20,24},{24,20},{28,16},{1,13},{... | collective-permute-start | bytes 80 | tf_op jit(solution)/shard_map/ppermute | solution.py:54
  33.7 73.9 %all-to-all-start = ((bf16[8,6,256,128]{3,2,1,0:T(8,128)(2,1)}), bf16[8,6,256,128]{3,2,1,0:T(8,128)(2,1)}, u32[]{:S(2)}, u32[]{:S(2)}) async-start(bf16[8,6,256,128]{3,2,1,0:T(8,128)(2,1)} %bitcast.101), calls=%async_computation | async-start | bytes 6291456 | tf_op jit(solution)/shard_map/all_to_all | solution.py:57
  39.6 92.2 %all-reduce.3.cloned.1.call-start = ((), (), s32[]{:S(2)}) async-start(), calls=%async_computation.2 | async-start | bytes 131072 | tf_op jit(solution)/shard_map/psum | solution.py:33
  133.4 5.5 %copy-start.2 = (f32[128,128]{1,0:T(8,128)S(1)}, f32[128,128]{1,0:T(8,128)}, u32[]{:S(2)}) copy-start(f32[128,128]{1,0:T(8,128)} %all-reduce.3.cloned.1.call-done) | copy-start | bytes 196612
  141.5 5.7 %copy-start.1 = (f32[3,256,128]{1,2,0:T(8,128)S(1)}, f32[3,256,128]{1,2,0:T(8,128)}, u32[]{:S(2)}) copy-start(f32[3,256,128]{1,2,0:T(8,128)} %multiply_add_fusion.1) | copy-start | bytes 1179652
  168.9 141.3 %all-to-all-start.1 = ((f32[8,6,256,128]{3,2,1,0:T(8,128)}), f32[8,6,256,128]{3,2,1,0:T(8,128)}, u32[]{:S(2)}, u32[]{:S(2)}) async-start(f32[8,6,256,128]{3,2,1,0:T(8,128)} %bitcast.99), calls=%async_computation.1 | async-start | bytes 12582912 | tf_op jit(solution)/shard_map/all_to_all | solution.py:83
  173.6 232.0 %all-reduce.5.cloned.1.call-start = ((), (), s32[]{:S(2)}) async-start(), calls=%async_computation.3 | async-start | bytes 8388608 | tf_op jit(solution)/shard_map/psum | solution.py:99
Sparse Core Ops, SparseCore 0:
  44.4 87.3 all-reduce.2
  321.2 84.4 all-reduce.4
